TPU v7x, 32 devices: a whole 2x2x4 slice. The times are simulated.
32 devices in a mesh: dp: 8 (over z, y), fsdp: 4 (over x, core).
Axes of the slice: x: 2, y: 2, z: 4, core: 2. Of those that a mesh axis runs over, the one named last changes fastest.
Arguments:
- hidden_in: bfloat16 [2, 32, 256, 768], P(None, ('dp', 'fsdp')), may hold values from -6 to 6
- patches: bfloat16 [2, 32, 2048, 768], P(None, ('dp', 'fsdp')), may hold values from -6 to 6
- token_segments: int32 [2, 32, 256], P(None, ('dp', 'fsdp')), may hold values from 0 to 3, as said below
- patch_segments: int32 [2, 32, 2048], P(None, ('dp', 'fsdp')), may hold values from 0 to 3, as said below
- cotangent: bfloat16 [2, 32, 256, 768], P(None, ('dp', 'fsdp')), may hold values from -6 to 6
- attention_weights: float32 [8, 768, 768], P(None, 'fsdp', 'dp'), may hold values from -1.1547005 to 1.1547005
- attention_means: float32 [8, 768, 768], P(None, 'fsdp', 'dp'), may hold values from -40 to 40
- attention_squares: float32 [8, 768, 768], P(None, 'fsdp', 'dp'), may hold values from 131.072 to 1638.4
- inner_weights: float32 [2, 768, 2048], P(None, 'fsdp', 'dp'), may hold values from -0.21875 to 0.21875
- inner_means: float32 [2, 768, 2048], P(None, 'fsdp', 'dp'), may hold values from -40 to 40
- inner_squares: float32 [2, 768, 2048], P(None, 'fsdp', 'dp'), may hold values from 131.072 to 1638.4
- outer_weights: float32 [2048, 768], P('fsdp', 'dp'), may hold values from -0.125 to 0.125
- outer_means: float32 [2048, 768], P('fsdp', 'dp'), may hold values from -48 to 48
- outer_squares: float32 [2048, 768], P('fsdp', 'dp'), may hold values from 163.84 to 2457.6
- norm_gains: float32 [3, 768], P(None, 'fsdp'), may hold values from 0.25 to 1.75
- gain_means: float32 [3, 768], P(None, 'fsdp'), may hold values from -80 to 80
- gain_squares: float32 [3, 768], P(None, 'fsdp'), may hold values from 425.984 to 6881.28
Outputs:
- hidden_out: bfloat16 [2, 32, 256, 768], P(None, ('dp', 'fsdp'))
- hidden_grad: float32 [2, 32, 256, 768], P(None, ('dp', 'fsdp'))
- patch_grad: float32 [2, 32, 2048, 768], P(None, ('dp', 'fsdp'))
- attention_mean: float32 [8, 768, 768], P(None, 'fsdp', 'dp')
- attention_square: float32 [8, 768, 768], P(None, 'fsdp', 'dp')
- attention_master: float32 [8, 768, 768], P(None, 'fsdp', 'dp')
- attention_copy: bfloat16 [8, 768, 768], P(None, 'fsdp', 'dp')
- inner_mean: float32 [2, 768, 2048], P(None, 'fsdp', 'dp')
- inner_square: float32 [2, 768, 2048], P(None, 'fsdp', 'dp')
- inner_master: float32 [2, 768, 2048], P(None, 'fsdp', 'dp')
- inner_copy: bfloat16 [2, 768, 2048], P(None, 'fsdp', 'dp')
- outer_mean: float32 [2048, 768], P('fsdp', 'dp')
- outer_square: float32 [2048, 768], P('fsdp', 'dp')
- outer_master: float32 [2048, 768], P('fsdp', 'dp')
- outer_copy: bfloat16 [2048, 768], P('fsdp', 'dp')
- gain_mean: float32 [3, 768], P(None, 'fsdp')
- gain_square: float32 [3, 768], P(None, 'fsdp')
- gain_master: float32 [3, 768], P(None, 'fsdp')
- gain_copy: bfloat16 [3, 768], P(None, 'fsdp')
Inputs may be any that keep to these rules, and one draw needn't show every extreme that they name: `token_segments`: along each row the ids never fall from one token to the next, and each of the 4 ids holds one token or more. `patch_segments`: along each row the ids never fall from one patch to the next, and each of the 4 ids holds one patch or more.
All inputs are finite; a program needn't handle non-finite values.
Results may differ from a plain program's by a relative error of at most 0.02.
The roundings to bfloat16 on the way count: a program that leaves them out, or rounds other values in their place, can miss the bound.
Values may be sent and summed in bfloat16 or wider, within the bound.
A program may use at most 320 MiB of HBM per device.

v0:
```python
import jax
import jax.numpy as jnp
from jax import lax
from jax.sharding import PartitionSpec as P

D = 768
HEADS = 12
HEAD = 64
STEP = 10
epsilon = 1e-06
score_scale = 0.125
masked_value = -1000000000.0
beta_one = 0.9
beta_two = 0.95
adam_epsilon = 1e-08
decay_matrix = 0.1
rate_matrix = 0.1
rate_gain = 0.3
float_type = jnp.float32
brain_type = jnp.bfloat16


def gelu_tanh(values):
    return (
        0.5
        * values
        * (1.0 + jnp.tanh(0.7978845608028654 * (values + 0.044715 * values * values * values)))
    )


def split_heads(matrix):
    return matrix.reshape(matrix.shape[:-1] + (HEADS, HEAD))


def norm_forward(values, gain):
    inverse_rms = lax.rsqrt(jnp.mean(values * values, axis=-1, keepdims=True) + epsilon)
    unit_rows = values * inverse_rms
    return (unit_rows * gain.astype(float_type), unit_rows, inverse_rms)


def norm_backward(grad_rows, gain, unit_rows, inverse_rms):
    grad_unit = grad_rows * gain.astype(float_type)
    grad_values = inverse_rms * (
        grad_unit - unit_rows * jnp.mean(grad_unit * unit_rows, axis=-1, keepdims=True)
    )
    return (grad_values, jnp.sum(grad_rows * unit_rows, axis=0))


def softmax_rows(scores):
    row_maximum = jnp.max(scores, axis=-1, keepdims=True)
    raised = jnp.exp(scores - row_maximum)
    return raised / jnp.sum(raised, axis=-1, keepdims=True)


def attend_forward(queries, key_heads, value_heads, allowed):
    scores = score_scale * jnp.einsum(
        "qhe,khe->hqk", queries, key_heads, preferred_element_type=float_type
    )
    probabilities = softmax_rows(jnp.where(allowed[None], scores, masked_value))
    rounded_probs = probabilities.astype(brain_type)
    mixture = jnp.einsum(
        "hqk,khe->qhe", rounded_probs, value_heads, preferred_element_type=float_type
    )
    return (mixture.astype(brain_type), probabilities, rounded_probs)


def attend_backward(grad_mixture, queries, key_heads, value_heads, probabilities, rounded_probs):
    grad_probs = jnp.einsum(
        "qhe,khe->hqk", grad_mixture, value_heads, preferred_element_type=float_type
    )
    grad_values = jnp.einsum(
        "hqk,qhe->khe", rounded_probs, grad_mixture, preferred_element_type=float_type
    ).astype(brain_type)
    row_inner = jnp.sum(probabilities * grad_probs, axis=-1, keepdims=True)
    grad_scores = (probabilities * (grad_probs - row_inner)).astype(brain_type)
    grad_queries = (
        score_scale
        * jnp.einsum("hqk,khe->qhe", grad_scores, key_heads, preferred_element_type=float_type)
    ).astype(brain_type)
    grad_keys = (
        score_scale
        * jnp.einsum("hqk,qhe->khe", grad_scores, queries, preferred_element_type=float_type)
    ).astype(brain_type)
    return (grad_queries, grad_keys, grad_values)


def layer_forward(weights, hidden, patch_rows, token_ids, patch_ids):
    attention, inner_matrix, outer_matrix, gain_rows = weights
    length = hidden.shape[0]
    initial = hidden.astype(float_type)
    normed_one, unit_one, rms_one = norm_forward(initial, gain_rows[0])
    normed_one = normed_one.astype(brain_type)
    projected = jnp.einsum(
        "nd,kde->kne", normed_one, attention[0:3], preferred_element_type=float_type
    ).astype(brain_type)
    heads_in = split_heads(projected)
    places = jnp.arange(length)
    causal = (places[:, None] >= places[None, :]) & (token_ids[:, None] == token_ids[None, :])
    mixture_one, probs_one, rounded_one = attend_forward(
        heads_in[0], heads_in[1], heads_in[2], causal
    )
    mixture_one = mixture_one.reshape(length, D)
    after_one = initial + jnp.dot(mixture_one, attention[3], preferred_element_type=float_type)
    normed_two, unit_two, rms_two = norm_forward(after_one, gain_rows[1])
    normed_two = normed_two.astype(brain_type)
    cross_query = split_heads(
        jnp.dot(normed_two, attention[4], preferred_element_type=float_type).astype(brain_type)
    )
    cross_pair = split_heads(
        jnp.einsum(
            "pd,kde->kpe", patch_rows, attention[5:7], preferred_element_type=float_type
        ).astype(brain_type)
    )
    matching = token_ids[:, None] == patch_ids[None, :]
    mixture_two, probs_two, rounded_two = attend_forward(
        cross_query, cross_pair[0], cross_pair[1], matching
    )
    mixture_two = mixture_two.reshape(length, D)
    after_two = after_one + jnp.dot(mixture_two, attention[7], preferred_element_type=float_type)
    normed_three, unit_three, rms_three = norm_forward(after_two, gain_rows[2])
    normed_three = normed_three.astype(brain_type)
    gated = jnp.einsum("nd,kdf->knf", normed_three, inner_matrix, preferred_element_type=float_type)
    units = (gelu_tanh(gated[0]) * gated[1]).astype(brain_type)
    layer_out = (
        after_two + jnp.dot(units, outer_matrix, preferred_element_type=float_type)
    ).astype(brain_type)
    stored = {
        "unit_one": unit_one,
        "rms_one": rms_one,
        "normed_one": normed_one,
        "heads_in": heads_in,
        "probs_one": probs_one,
        "rounded_one": rounded_one,
        "mixture_one": mixture_one,
        "unit_two": unit_two,
        "rms_two": rms_two,
        "normed_two": normed_two,
        "cross_query": cross_query,
        "cross_pair": cross_pair,
        "probs_two": probs_two,
        "rounded_two": rounded_two,
        "mixture_two": mixture_two,
        "unit_three": unit_three,
        "rms_three": rms_three,
        "normed_three": normed_three,
        "gated": gated,
        "units": units,
    }
    return (layer_out, stored)


def layer_backward(weights, stored, cotangent_row, patch_rows):
    attention, inner_matrix, outer_matrix, gain_rows = weights
    length = cotangent_row.shape[0]
    grad_final = cotangent_row.astype(float_type)
    grad_low = grad_final.astype(brain_type)
    grad_outer = jnp.einsum(
        "nf,nd->fd", stored["units"], grad_low, preferred_element_type=float_type
    )
    grad_units = jnp.einsum("nd,fd->nf", grad_low, outer_matrix, preferred_element_type=float_type)
    gate_in = stored["gated"][0]
    up_in = stored["gated"][1]
    activation, gelu_back = jax.vjp(gelu_tanh, gate_in)
    grad_gate = gelu_back(grad_units * up_in)[0]
    grad_gated = jnp.stack([grad_gate, grad_units * activation]).astype(brain_type)
    grad_inner = jnp.einsum(
        "nd,knf->kdf", stored["normed_three"], grad_gated, preferred_element_type=float_type
    )
    grad_normed = jnp.einsum(
        "knf,kdf->nd", grad_gated, inner_matrix, preferred_element_type=float_type
    )
    grad_from_three, gain_three = norm_backward(
        grad_normed, gain_rows[2], stored["unit_three"], stored["rms_three"]
    )
    grad_after_two = grad_final + grad_from_three
    branch_two = grad_after_two.astype(brain_type)
    grad_cross_out = jnp.einsum(
        "nd,ne->de", stored["mixture_two"], branch_two, preferred_element_type=float_type
    )
    grad_mixture_two = split_heads(
        jnp.einsum("ne,de->nd", branch_two, attention[7], preferred_element_type=float_type).astype(
            brain_type
        )
    )
    cross_pair = stored["cross_pair"]
    grad_cq, grad_ck, grad_cv = attend_backward(
        grad_mixture_two,
        stored["cross_query"],
        cross_pair[0],
        cross_pair[1],
        stored["probs_two"],
        stored["rounded_two"],
    )
    grad_cq = grad_cq.reshape(length, D)
    grad_pair = jnp.stack([grad_ck, grad_cv]).reshape(2, patch_rows.shape[0], D)
    grad_cross_query = jnp.einsum(
        "nd,ne->de", stored["normed_two"], grad_cq, preferred_element_type=float_type
    )
    grad_cross_pair = jnp.einsum(
        "pd,kpe->kde", patch_rows, grad_pair, preferred_element_type=float_type
    )
    patch_grad = jnp.einsum(
        "kpe,kde->pd", grad_pair, attention[5:7], preferred_element_type=float_type
    )
    grad_normed_two = jnp.einsum(
        "ne,de->nd", grad_cq, attention[4], preferred_element_type=float_type
    )
    grad_from_two, gain_two = norm_backward(
        grad_normed_two, gain_rows[1], stored["unit_two"], stored["rms_two"]
    )
    grad_after_one = grad_after_two + grad_from_two
    branch_one = grad_after_one.astype(brain_type)
    grad_self_out = jnp.einsum(
        "nd,ne->de", stored["mixture_one"], branch_one, preferred_element_type=float_type
    )
    grad_mixture_one = split_heads(
        jnp.einsum("ne,de->nd", branch_one, attention[3], preferred_element_type=float_type).astype(
            brain_type
        )
    )
    heads_in = stored["heads_in"]
    grad_query, grad_key, grad_value = attend_backward(
        grad_mixture_one,
        heads_in[0],
        heads_in[1],
        heads_in[2],
        stored["probs_one"],
        stored["rounded_one"],
    )
    grad_projected = jnp.stack([grad_query, grad_key, grad_value]).reshape(3, length, D)
    grad_self_in = jnp.einsum(
        "nd,kne->kde", stored["normed_one"], grad_projected, preferred_element_type=float_type
    )
    grad_normed_one = jnp.einsum(
        "kne,kde->nd", grad_projected, attention[0:3], preferred_element_type=float_type
    )
    grad_from_one, gain_one = norm_backward(
        grad_normed_one, gain_rows[0], stored["unit_one"], stored["rms_one"]
    )
    hidden_grad = grad_after_one + grad_from_one
    grad_attention = jnp.concatenate(
        [
            grad_self_in,
            grad_self_out[None],
            grad_cross_query[None],
            grad_cross_pair,
            grad_cross_out[None],
        ],
        axis=0,
    )
    grad_gains = jnp.stack([gain_one, gain_two, gain_three])
    return (hidden_grad, patch_grad, (grad_attention, grad_inner, grad_outer, grad_gains))


def fetch_forward(copies):
    widened = (
        lax.all_gather(copies[0], "fsdp", axis=1, tiled=True),
        lax.all_gather(copies[1], "fsdp", axis=1, tiled=True),
        lax.all_gather(copies[2], "fsdp", axis=0, tiled=True),
        lax.all_gather(copies[3], "fsdp", axis=1, tiled=True),
    )
    complete = (
        lax.all_gather(widened[0], "dp", axis=2, tiled=True),
        lax.all_gather(widened[1], "dp", axis=2, tiled=True),
        lax.all_gather(widened[2], "dp", axis=1, tiled=True),
    )
    return (complete[0], complete[1], complete[2], widened[3])


def fetch_backward(copies):
    widened = (
        lax.all_gather(copies[0], "fsdp", axis=1, tiled=True),
        lax.all_gather(copies[1], "fsdp", axis=1, tiled=True),
        lax.all_gather(copies[2], "fsdp", axis=0, tiled=True),
        lax.all_gather(copies[3], "fsdp", axis=1, tiled=True),
    )
    complete = (
        lax.all_gather(widened[0], "dp", axis=2, tiled=True),
        lax.all_gather(widened[1], "dp", axis=2, tiled=True),
        lax.all_gather(widened[2], "dp", axis=1, tiled=True),
    )
    return (complete[0], complete[1], complete[2], widened[3])


def reduce_grads(totals):
    partial_sums = (
        lax.psum_scatter(totals[0], "dp", scatter_dimension=2, tiled=True),
        lax.psum_scatter(totals[1], "dp", scatter_dimension=2, tiled=True),
        lax.psum_scatter(totals[2], "dp", scatter_dimension=1, tiled=True),
    )
    gain_totals = lax.psum(totals[3], "dp")
    return (
        lax.psum_scatter(partial_sums[0], "fsdp", scatter_dimension=1, tiled=True),
        lax.psum_scatter(partial_sums[1], "fsdp", scatter_dimension=1, tiled=True),
        lax.psum_scatter(partial_sums[2], "fsdp", scatter_dimension=0, tiled=True),
        lax.psum_scatter(gain_totals, "fsdp", scatter_dimension=1, tiled=True),
    )


def adam_update(weight, mean_old, square_old, gradient, step_rate, decay_rate):
    mean_new = beta_one * mean_old + (1.0 - beta_one) * gradient
    square_new = beta_two * square_old + (1.0 - beta_two) * gradient * gradient
    corrected = (
        mean_new
        / (1.0 - beta_one**STEP)
        / (jnp.sqrt(square_new / (1.0 - beta_two**STEP)) + adam_epsilon)
    )
    master = weight - step_rate * (corrected + decay_rate * weight)
    return (mean_new, square_new, master, master.astype(jnp.bfloat16))


def on_device(
    hidden_in,
    patches,
    token_segments,
    patch_segments,
    cotangent,
    attention_weights,
    attention_means,
    attention_squares,
    inner_weights,
    inner_means,
    inner_squares,
    outer_weights,
    outer_means,
    outer_squares,
    norm_gains,
    gain_means,
    gain_squares,
):
    copies = (
        attention_weights.astype(brain_type),
        inner_weights.astype(brain_type),
        outer_weights.astype(brain_type),
        norm_gains.astype(brain_type),
    )
    layer_outputs = []
    input_grads = []
    patch_grads = []
    totals = None
    for batch_index in range(hidden_in.shape[0]):
        forward_weights = fetch_forward(copies)
        layer_out, stored = layer_forward(
            forward_weights,
            hidden_in[batch_index, 0],
            patches[batch_index, 0],
            token_segments[batch_index, 0],
            patch_segments[batch_index, 0],
        )
        backward_weights = fetch_backward(copies)
        hidden_grad, patch_grad, gradients = layer_backward(
            backward_weights, stored, cotangent[batch_index, 0], patches[batch_index, 0]
        )
        layer_outputs.append(layer_out)
        input_grads.append(hidden_grad)
        patch_grads.append(patch_grad)
        totals = gradients if totals is None else jax.tree.map(jnp.add, totals, gradients)
    owned_grads = reduce_grads(totals)
    attention_new = adam_update(
        attention_weights,
        attention_means,
        attention_squares,
        owned_grads[0],
        rate_matrix,
        decay_matrix,
    )
    inner_new = adam_update(
        inner_weights, inner_means, inner_squares, owned_grads[1], rate_matrix, decay_matrix
    )
    outer_new = adam_update(
        outer_weights, outer_means, outer_squares, owned_grads[2], rate_matrix, decay_matrix
    )
    gain_new = adam_update(norm_gains, gain_means, gain_squares, owned_grads[3], rate_gain, 0.0)
    hidden_out = jnp.stack(layer_outputs)[:, None]
    hidden_grads = jnp.stack(input_grads)[:, None]
    patch_grads_all = jnp.stack(patch_grads)[:, None]
    return (
        hidden_out,
        hidden_grads,
        patch_grads_all,
        attention_new[0],
        attention_new[1],
        attention_new[2],
        attention_new[3],
        inner_new[0],
        inner_new[1],
        inner_new[2],
        inner_new[3],
        outer_new[0],
        outer_new[1],
        outer_new[2],
        outer_new[3],
        gain_new[0],
        gain_new[1],
        gain_new[2],
        gain_new[3],
    )


def solution(mesh):
    placed = (
        P(None, ("dp", "fsdp"), None, None),
        P(None, ("dp", "fsdp"), None, None),
        P(None, ("dp", "fsdp"), None),
        P(None, ("dp", "fsdp"), None),
        P(None, ("dp", "fsdp"), None, None),
        P(None, "fsdp", "dp"),
        P(None, "fsdp", "dp"),
        P(None, "fsdp", "dp"),
        P(None, "fsdp", "dp"),
        P(None, "fsdp", "dp"),
        P(None, "fsdp", "dp"),
        P("fsdp", "dp"),
        P("fsdp", "dp"),
        P("fsdp", "dp"),
        P(None, "fsdp"),
        P(None, "fsdp"),
        P(None, "fsdp"),
    )
    return jax.shard_map(
        on_device,
        mesh=mesh,
        in_specs=placed,
        out_specs=(
            P(None, ("dp", "fsdp"), None, None),
            P(None, ("dp", "fsdp"), None, None),
            P(None, ("dp", "fsdp"), None, None),
            P(None, "fsdp", "dp"),
            P(None, "fsdp", "dp"),
            P(None, "fsdp", "dp"),
            P(None, "fsdp", "dp"),
            P(None, "fsdp", "dp"),
            P(None, "fsdp", "dp"),
            P(None, "fsdp", "dp"),
            P(None, "fsdp", "dp"),
            P("fsdp", "dp"),
            P("fsdp", "dp"),
            P("fsdp", "dp"),
            P("fsdp", "dp"),
            P(None, "fsdp"),
            P(None, "fsdp"),
            P(None, "fsdp"),
            P(None, "fsdp"),
        ),
        check_vma=False,
    )
```

profile of v0, /device:TPU:0, one launch (start us, length us, event | category | flops | bytes accessed | tf_op | source)
XLA Modules:
  0.0 1277.1 jit_solution(9727439426056397318)
XLA Ops:
  9.8 22.8 %all-gather.6.cloned.1.call-done = bf16[8,768,96]{2,0,1:T(8,128)(2,1)} async-done(((bf16[8,192,96]{2,0,1:T(8,128)(2,1)}), bf16[8,768,96]{2,0,1:T(8,128)(2,1)}) %all-gather.6.cloned.1.call-update) | async-done | bytes 1179664 | tf_op jit(solution)/shard_map/all_gather | solution.py:257
  35.8 9.0 all_gather.17
  54.9 118.2 %all-gather.8.cloned.1.call-done = bf16[8,768,768]{1,0,2:T(8,128)(2,1)} async-done(((bf16[8,768,96]{1,0,2:T(8,128)(2,1)}), bf16[8,768,768]{1,0,2:T(8,128)(2,1)}) %all-gather.8.cloned.1.call-update) | async-done | bytes 9437200 | tf_op jit(solution)/shard_map/all_gather | solution.py:263
  188.5 18.3 %fusion.261 = (bf16[1,768,768]{1,0,2:T(2,128)(2,1)}, bf16[1,768,768]{1,0,2:T(2,128)(2,1)}, bf16[1,768,768]{1,0,2:T(2,128)(2,1)}) fusion(bf16[8,768,768]{1,0,2:T(8,128)(2,1)} %all-gather.8.cloned.1.call-done), kind=kLoop, calls=%fused_computation.380 | loop fusion | bytes 7077888 | tf_op jit(solution)/shard_map/slice | solution.py:119
  265.6 14.4 %fusion.271 = (f32[12,256]{1,0:T(8,128)S(1)}, f32[12,256,2048]{2,1,0:T(8,128)}) fusion(pred[256,2048]{1,0:T(8,128)(4,1)} %broadcast_compare_fusion.1, bf16[256,12,64]{0,2,1:T(8,128)(2,1)S(1)} %bitcast.442, bf16[2048,12,64]{0,2,1:T(8,128)(2,1)} %bitcast.427), kind=kOutput, calls=%fused_computation.390 | convolution fusion | flops 830474240 | bytes 29241344 | tf_op jit(solution)/shard_map/sub | solution.py:51
  287.0 11.6 fusion.101
  311.3 14.4 %fusion.269 = (f32[12,256]{1,0:T(8,128)S(1)}, f32[12,256,2048]{2,1,0:T(8,128)}) fusion(pred[256,2048]{1,0:T(8,128)(4,1)} %broadcast_compare_fusion, bf16[256,12,64]{0,2,1:T(8,128)(2,1)S(1)} %bitcast.444, bf16[2048,12,64]{0,2,1:T(8,128)(2,1)} %bitcast.429), kind=kOutput, calls=%fused_computation.388 | convolution fusion | flops 830474240 | bytes 29241344 | tf_op jit(solution)/shard_map/sub | solution.py:51
  325.8 11.5 fusion.104
  355.5 116.4 %reduce-scatter.15.cloned.1.call-done = f32[2048,96]{0,1:T(8,128)} async-done(((f32[2048,768]{0,1:T(8,128)}), f32[2048,96]{0,1:T(8,128)}) %reduce-scatter.15.cloned.1.call-update) | async-done | bytes 786448 | tf_op jit(solution)/shard_map/reduce_scatter | solution.py:289
  471.9 24.8 %reduce-scatter.17.cloned.1.call-done = f32[512,96]{0,1:T(8,128)} async-done(((f32[2048,96]{0,1:T(8,128)}), f32[512,96]{0,1:T(8,128)}) %reduce-scatter.17.cloned.1.call-update) | async-done | bytes 196624 | tf_op jit(solution)/shard_map/reduce_scatter | solution.py:295
  505.6 60.4 %all-gather.12.cloned.1.call-done = bf16[2048,768]{0,1:T(8,128)(2,1)} async-done(((bf16[2048,96]{0,1:T(8,128)(2,1)}), bf16[2048,768]{0,1:T(8,128)(2,1)}) %all-gather.12.cloned.1.call-update) | async-done | bytes 3145744 | tf_op jit(solution)/shard_map/all_gather | solution.py:265
  591.4 11.2 fusion.29
  602.6 18.0 %multiply_reduce_fusion = (f32[12,256]{1,0:T(8,128)}, f32[12,256,2048]{2,1,0:T(8,128)}) fusion(f32[12,256,2048]{2,1,0:T(8,128)} %get-tuple-element.202, f32[12,256]{1,0:T(8,128)} %copy-done.110, bf16[256,12,64]{0,2,1:T(8,128)(2,1)} %bitcast.478, bf16[2048,12,64]{0,2,1:T(8,128)(2,1)} %bitcast.441), kind=kOutput, calls=%fused_computation.5 | convolution fusion | flops 824177664 | bytes 53895168 | tf_op jit(solution)/shard_map/qhe,khe->hqk/dot_general | solution.py:68
  621.4 11.8 add_bitcast_fusion
  633.9 12.0 fusion.26
  653.6 16.7 %multiply_convert_fusion = bf16[12,256,2048]{2,1,0:T(8,128)(2,1)S(1)} fusion(f32[12,256,2048]{2,1,0:T(8,128)} %get-tuple-element.215, f32[12,256]{1,0:T(8,128)} %get-tuple-element.214, f32[12,256,2048]{2,1,0:T(8,128)} %get-tuple-element.202, f32[12,256]{1,0:T(8,128)} %copy-done.110), kind=kLoop, calls=%fused_computation.4 | loop fusion | flops 25165824 | bytes 62939136 | tf_op jit(solution)/shard_map/convert_element_type | solution.py:75
  677.7 17.6 %multiply_reduce_fusion.1 = (f32[12,256]{1,0:T(8,128)S(1)}, f32[12,256,2048]{2,1,0:T(8,128)}) fusion(f32[12,256,2048]{2,1,0:T(8,128)} %get-tuple-element.208, f32[12,256]{1,0:T(8,128)S(1)} %copy-done.109, bf16[256,12,64]{0,2,1:T(8,128)(2,1)S(1)} %bitcast.472, bf16[2048,12,64]{0,2,1:T(8,128)(2,1)} %bitcast.439), kind=kOutput, calls=%fused_computation.7 | convolution fusion | flops 824177664 | bytes 53895168 | tf_op jit(solution)/shard_map/qhe,khe->hqk/dot_general | solution.py:68
  695.3 16.5 %multiply_convert_fusion.1 = bf16[12,256,2048]{2,1,0:T(8,128)(2,1)S(1)} fusion(f32[12,256,2048]{2,1,0:T(8,128)} %get-tuple-element.217, f32[12,256]{1,0:T(8,128)S(1)} %get-tuple-element.216, f32[12,256,2048]{2,1,0:T(8,128)} %get-tuple-element.208, f32[12,256]{1,0:T(8,128)S(1)} %copy-done.109), kind=kLoop, calls=%fused_computation.6 | loop fusion | flops 25165824 | bytes 62939136 | tf_op jit(solution)/shard_map/convert_element_type | solution.py:75
  719.9 9.8 fusion.99
  812.3 13.1 %add.227 = f32[8,768,768]{1,2,0:T(8,128)} add(f32[8,768,768]{1,2,0:T(8,128)} %bitcast_dynamic-update-slice_fusion.7, f32[8,768,768]{1,2,0:T(8,128)S(1)} %bitcast_dynamic-update-slice_fusion.4) | non-fusion elementwise | flops 4718592 | bytes 56623104 | tf_op jit(solution)/shard_map/add | solution.py:357
  855.0 299.2 %reduce-scatter.11.cloned.1.call-done = f32[8,768,96]{1,2,0:T(8,128)} async-done(((f32[8,768,768]{1,2,0:T(8,128)}), f32[8,768,96]{1,2,0:T(8,128)}) %reduce-scatter.11.cloned.1.call-update) | async-done | bytes 2359312 | tf_op jit(solution)/shard_map/reduce_scatter | solution.py:287
  1184.6 9.1 maximum_bitcast_fusion
  1194.7 19.9 %psum.8 = f32[3,192]{1,0:T(4,128)S(1)} all-reduce(f32[3,192]{1,0:T(4,128)S(1)} %copy.478), channel_id=1, replica_groups=mesh['dp'=8,'fsdp'=4] {'dp'}, use_global_device_ids=true, to_apply=%region_36.37 | all-reduce | flops 576 | bytes 4608 | tf_op jit(solution)/shard_map/psum | solution.py:291
  1226.0 31.7 %reduce-scatter.19.cloned.1.call-done = f32[192,768]{1,0:T(8,128)} async-done(((f32[768,768]{1,0:T(8,128)}), f32[192,768]{1,0:T(8,128)}) %reduce-scatter.19.cloned.1.call-update) | async-done | bytes 589840
  (449 shorter events, 351.9 us)
Async XLA Ops:
  7.2 25.3 %all-gather.6.cloned.1.call-start = ((), (), s32[]{:S(2)}) async-start(), calls=%async_computation.6 | async-start | bytes 1966080 | tf_op jit(solution)/shard_map/all_gather | solution.py:257
  9.7 41.4 %copy-start.113 = (s32[2,1,2048]{2,1,0:T(1,128)S(1)}, s32[2,1,2048]{2,1,0:T(1,128)}, u32[]{:S(2)}) copy-start(s32[2,1,2048]{2,1,0:T(1,128)} %param.20) | copy-start | bytes 49156
  9.7 163.5 %all-gather.8.cloned.1.call-start = ((), (), s32[]{:S(2)}) async-start(), calls=%async_computation.7 | async-start | bytes 10616832 | tf_op jit(solution)/shard_map/all_gather | solution.py:263
  35.8 302.3 %all-gather.10.cloned.1.call-start = ((), (), s32[]{:S(2)}) async-start(), calls=%async_computation.8 | async-start | bytes 7077888 | tf_op jit(solution)/shard_map/all_gather | solution.py:264
  44.9 427.0 %reduce-scatter.15.cloned.1.call-start = ((), (), s32[]{:S(2)}) async-start(), calls=%async_computation.12 | async-start | bytes 7077888 | tf_op jit(solution)/shard_map/reduce_scatter | solution.py:289
  51.1 175.6 %copy-start.115 = (f32[768]{0:T(1024)}, f32[768]{0:T(1024)S(1)}, u32[]{:S(2)}) copy-start(f32[768]{0:T(1024)S(1)} %get-tuple-element.151) | copy-start | bytes 9220
  51.1 228.9 %copy-start.99 = (f32[768]{0:T(1024)}, f32[768]{0:T(1024)S(1)}, u32[]{:S(2)}) copy-start(f32[768]{0:T(1024)S(1)} %get-tuple-element.150) | copy-start | bytes 9220
  54.9 163.0 %copy-start.121 = (f32[256]{0:T(256)}, f32[256]{0:T(256)S(1)}, u32[]{:S(2)}) copy-start(f32[256]{0:T(256)S(1)} %get-tuple-element.225) | copy-start | bytes 3076
  54.9 171.8 %copy-start.123 = (f32[256]{0:T(256)}, f32[256]{0:T(256)S(1)}, u32[]{:S(2)}) copy-start(f32[256]{0:T(256)S(1)} %get-tuple-element.226) | copy-start | bytes 3076
  217.9 62.2 %copy-start.4 = (bf16[1,768,768]{2,1,0:T(8,128)(2,1)}, bf16[1,768,768]{2,1,0:T(8,128)(2,1)S(1)}, u32[]{:S(2)}) copy-start(bf16[1,768,768]{2,1,0:T(8,128)(2,1)S(1)} %copy.482) | copy-start | bytes 3538948
  241.7 56.9 %copy-start.8 = (f32[256,768]{1,0:T(8,128)}, f32[256,768]{1,0:T(8,128)S(1)}, u32[]{:S(2)}) copy-start(f32[256,768]{1,0:T(8,128)S(1)} %get-tuple-element.206) | copy-start | bytes 2359300
  249.7 87.6 %copy-start.10 = (f32[256,768]{1,0:T(8,128)}, f32[256,768]{1,0:T(8,128)S(1)}, u32[]{:S(2)}) copy-start(f32[256,768]{1,0:T(8,128)S(1)} %get-tuple-element.200) | copy-start | bytes 2359300
  299.2 289.5 %copy-start.12 = (f32[256,768]{1,0:T(8,128)}, f32[256,768]{1,0:T(8,128)S(1)}, u32[]{:S(2)}) copy-start(f32[256,768]{1,0:T(8,128)S(1)} %get-tuple-element.210) | copy-start | bytes 2359300
  338.1 283.3 %copy-start.14 = (f32[256,768]{1,0:T(8,128)}, f32[256,768]{1,0:T(8,128)S(1)}, u32[]{:S(2)}) copy-start(f32[256,768]{1,0:T(8,128)S(1)} %get-tuple-element.212) | copy-start | bytes 2359300
  355.5 141.3 %reduce-scatter.17.cloned.1.call-start = ((), (), s32[]{:S(2)}) async-start(), calls=%async_computation.13 | async-start | bytes 983040 | tf_op jit(solution)/shard_map/reduce_scatter | solution.py:295
  471.9 94.1 %all-gather.12.cloned.1.call-start = ((), (), s32[]{:S(2)}) async-start(), calls=%async_computation.9 | async-start | bytes 3538944 | tf_op jit(solution)/shard_map/all_gather | solution.py:265
  505.5 333.9 %reduce-scatter.13.cloned.1.call-start = ((), (), s32[]{:S(2)}) async-start(), calls=%async_computation.11 | async-start | bytes 14155776 | tf_op jit(solution)/shard_map/reduce_scatter | solution.py:288
  633.2 521.0 %reduce-scatter.11.cloned.1.call-start = ((), (), s32[]{:S(2)}) async-start(), calls=%async_computation.10 | async-start | bytes 21233664 | tf_op jit(solution)/shard_map/reduce_scatter | solution.py:287
  825.4 368.3 %reduce-scatter.21.cloned.1.call-start = ((), (), s32[]{:S(2)}) async-start(), calls=%async_computation.15 | async-start | bytes 491520
  833.6 388.7 %all-reduce.3.cloned.1.call-start = ((), (), s32[]{:S(2)}) async-start(), calls=%async_computation.16 | async-start | bytes 3145728
  843.1 414.7 %reduce-scatter.19.cloned.1.call-start = ((), (), s32[]{:S(2)}) async-start(), calls=%async_computation.14 | async-start | bytes 2949120
  1184.6 38.9 %copy-start.76 = (f32[2,192,256]{2,1,0:T(8,128)S(1)}, f32[2,192,256]{2,1,0:T(8,128)}, u32[]{:S(2)}) copy-start(f32[2,192,256]{2,1,0:T(8,128)} %param.25) | copy-start | bytes 1179652
  1223.5 37.0 %copy-start.52 = (f32[8,192,96]{1,2,0:T(8,128)S(1)}, f32[8,192,96]{1,2,0:T(8,128)}, u32[]{:S(2)}) copy-start(f32[8,192,96]{1,2,0:T(8,128)} %copy.439) | copy-start | bytes 1769476
  1223.5 37.0 %copy-start.53 = (f32[8,192,96]{1,2,0:T(8,128)S(1)}, f32[8,192,96]{1,2,0:T(8,128)}, u32[]{:S(2)}) copy-start(f32[8,192,96]{1,2,0:T(8,128)} %copy.426) | copy-start | bytes 1769476
  (123 other events, 890.2 us)
Sparse Core Ops, SparseCore 0:
  10.1 22.3 all-gather.5
  35.9 137.2 all-gather.7
  175.2 97.6 all-gather.9
  355.6 116.2 reduce-scatter.14
  474.2 22.4 reduce-scatter.16
  505.7 60.2 all-gather.11
  633.3 206.0 reduce-scatter.12
  843.3 310.8 reduce-scatter.10
  1157.3 19.8 reduce-scatter.20
  1179.4 42.8 all-reduce.2
  1224.9 32.8 reduce-scatter.18
where the time goes:
time: 1280 us
  waiting for transfers between devices  686 us (54%)
  matrix products  296 us (23%)
  local copies, waits for them, and re-layouts  161 us (13%)
  other arithmetic  75.5 us (6%)
  blocking collectives  40.7 us (3%)
  between operations  16.7 us (1%)
    reduce_scatter x1, waiting for transfers between devices, reduce_grads(): lax.psum_scatter(totals[0], 'dp', scatter_dimension=2, tiled=True)  299 us
    all_gather x1, waiting for transfers between devices, fetch_forward(): lax.all_gather(widened[0], 'dp', axis=2, tiled=True)  118 us
    reduce_scatter x1, waiting for transfers between devices, reduce_grads(): lax.psum_scatter(totals[2], 'dp', scatter_dimension=1, tiled=True)  116 us
    unnamed x293, local copies, waits for them, and re-layouts  80.4 us
    all_gather x1, waiting for transfers between devices, fetch_forward(): lax.all_gather(widened[2], 'dp', axis=1, tiled=True)  60.4 us
    dot_general x4, matrix products, attend_backward(): jnp.einsum('qhe,khe->hqk', grad_mixture, value_heads, preferred_element_t...  41.4 us
    unnamed x14, waiting for transfers between devices  39 us
    sub x4, matrix products, softmax_rows(): raised = jnp.exp(scores - row_maximum)  37.1 us
  transfers between devices with their start and end apart: 11, of which 9 were waited for; matrix products, arithmetic and copies ran while one was open for 32% of the time, Pallas kernels for 0%

commit v1 on v0

--- a/solution.py
+++ b/solution.py
@@ -18,6 +18,19 @@
 rate_gain = 0.3
 float_type = jnp.float32
 brain_type = jnp.bfloat16
+
+
+def ring_gather(value, axis, dim):
+    ways = lax.axis_size(axis)
+    up = [(d, (d + 1) % ways) for d in range(ways)]
+    down = [(d, (d - 1) % ways) for d in range(ways)]
+    earlier, later = ([value], [value])
+    for _ in range(ways // 2):
+        earlier.append(lax.ppermute(earlier[-1], axis, up))
+    for _ in range((ways - 1) // 2):
+        later.append(lax.ppermute(later[-1], axis, down))
+    line = jnp.concatenate([*earlier[::-1], *later[1:]], axis=dim)
+    return jnp.roll(line, (lax.axis_index(axis) - ways // 2) * value.shape[dim], axis=dim)
 
 
 def gelu_tanh(values):
@@ -260,7 +273,7 @@
         lax.all_gather(copies[3], "fsdp", axis=1, tiled=True),
     )
     complete = (
-        lax.all_gather(widened[0], "dp", axis=2, tiled=True),
+        ring_gather(widened[0], "dp", 2),
         lax.all_gather(widened[1], "dp", axis=2, tiled=True),
         lax.all_gather(widened[2], "dp", axis=1, tiled=True),
     )

time: 1280 us -> 1390 us (1.086)
  waiting for transfers between devices: 686 us -> 760 us
  starting transfers between devices: 0.45 us -> 15.8 us
    ppermute x0 -> x7, waiting for transfers between devices: none -> 192 us  [the longest x4 192 us: ring_gather(): earlier.append(lax.ppermute(earlier[-1], axis, up))]
    unnamed x14, waiting for transfers between devices: 39 us -> 0.19 us
    all_gather x1, waiting for transfers between devices: 60.4 us -> 23.6 us  [fetch_forward(): lax.all_gather(widened[2], 'dp', axis=1, tiled=True)]
    reduce_scatter x1, waiting for transfers between devices: 299 us -> 276 us  [reduce_grads(): lax.psum_scatter(totals[0], 'dp', scatter_dimension=2, tiled=True)]
    ppermute x0 -> x7, starting transfers between devices: none -> 14.9 us  [the longest x3 7.55 us: ring_gather(): later.append(lax.ppermute(later[-1], axis, down))]
    unnamed x293 -> x301, local copies, waits for them, and re-layouts: 80.4 us -> 90.9 us
    slice x7 -> x3, local copies, waits for them, and re-layouts: 38.6 us -> 33.1 us  [the longest x1 18.4 us: layer_backward(): attention[3]]
  transfers between devices with their start and end apart: 11 -> 18, of which waited for: 9 -> 11; matrix products, arithmetic and copies ran while one was open for 32% -> 32% of each run, Pallas kernels for 0% -> 0%
where the time goes in v1:
time: 1390 us
  waiting for transfers between devices  760 us (55%)
  matrix products  301 us (22%)
  local copies, waits for them, and re-layouts  167 us (12%)
  other arithmetic  85 us (6%)
  blocking collectives  39.2 us (3%)
  between operations  18 us (1%)
  starting transfers between devices  15.8 us (1%)
    reduce_scatter x1, waiting for transfers between devices, reduce_grads(): lax.psum_scatter(totals[0], 'dp', scatter_dimension=2, tiled=True)  276 us
    ppermute x4, waiting for transfers between devices, ring_gather(): earlier.append(lax.ppermute(earlier[-1], axis, up))  192 us
    reduce_scatter x1, waiting for transfers between devices, reduce_grads(): lax.psum_scatter(totals[2], 'dp', scatter_dimension=1, tiled=True)  117 us
    all_gather x1, waiting for transfers between devices, fetch_backward(): lax.all_gather(widened[0], 'dp', axis=2, tiled=True)  108 us
    unnamed x301, local copies, waits for them, and re-layouts  90.9 us
    dot_general x4, matrix products, attend_backward(): jnp.einsum('qhe,khe->hqk', grad_mixture, value_heads, preferred_element_t...  41.2 us
    sub x4, matrix products, softmax_rows(): raised = jnp.exp(scores - row_maximum)  34.7 us
    convert_element_type x4, other arithmetic, attend_backward(): grad_scores = (probabilities * (grad_probs - row_inner)).astype(brain_type)  34.4 us
  transfers between devices with their start and end apart: 18, of which 11 were waited for; matrix products, arithmetic and copies ran while one was open for 32% of the time, Pallas kernels for 0%

profile of v1, /device:TPU:0, one launch (start us, length us, event | category | flops | bytes accessed | tf_op | source)
XLA Modules:
  0.0 1386.8 jit_solution(3651425688531886120)
XLA Ops:
  10.6 22.8 %all-gather.6.cloned.1.call-done = bf16[8,768,96]{2,0,1:T(8,128)(2,1)} async-done(((bf16[8,192,96]{2,0,1:T(8,128)(2,1)}), bf16[8,768,96]{2,0,1:T(8,128)(2,1)}) %all-gather.6.cloned.1.call-update) | async-done | bytes 1179664 | tf_op jit(solution)/shard_map/all_gather | solution.py:270
  37.0 29.3 %collective-permute-done = bf16[8,768,96]{1,2,0:T(8,128)(2,1)S(1)} collective-permute-done((bf16[8,768,96]{1,2,0:T(8,128)(2,1)S(1)}, bf16[8,768,96]{1,2,0:T(8,128)(2,1)S(1)}, u32[]{:S(2)}, u32[]{:S(2)}) %collective-permute-start) | collective-permute-done | bytes 1179680 | tf_op jit(solution)/shard_map/ppermute | solution.py:29
  84.4 40.7 %collective-permute-done.1 = bf16[8,768,96]{1,2,0:T(8,128)(2,1)} collective-permute-done((bf16[8,768,96]{1,2,0:T(8,128)(2,1)S(1)}, bf16[8,768,96]{1,2,0:T(8,128)(2,1)}, u32[]{:S(2)}, u32[]{:S(2)}) %collective-permute-start.1) | collective-permute-done | bytes 1179680 | tf_op jit(solution)/shard_map/ppermute | solution.py:29
  132.2 61.7 %collective-permute-done.2 = bf16[8,768,96]{1,2,0:T(8,128)(2,1)} collective-permute-done((bf16[8,768,96]{1,2,0:T(8,128)(2,1)}, bf16[8,768,96]{1,2,0:T(8,128)(2,1)}, u32[]{:S(2)}, u32[]{:S(2)}) %collective-permute-start.2) | collective-permute-done | bytes 1179680 | tf_op jit(solution)/shard_map/ppermute | solution.py:29
  201.6 60.1 %collective-permute-done.3 = bf16[8,768,96]{1,2,0:T(8,128)(2,1)} collective-permute-done((bf16[8,768,96]{1,2,0:T(8,128)(2,1)}, bf16[8,768,96]{1,2,0:T(8,128)(2,1)}, u32[]{:S(2)}, u32[]{:S(2)}) %collective-permute-start.3) | collective-permute-done | bytes 1179680 | tf_op jit(solution)/shard_map/ppermute | solution.py:29
  314.1 14.4 %fusion.262 = (f32[12,256]{1,0:T(8,128)S(1)}, f32[12,256,2048]{2,1,0:T(8,128)}) fusion(pred[256,2048]{1,0:T(8,128)(4,1)S(1)} %copy-done.79, bf16[256,12,64]{0,2,1:T(8,128)(2,1)S(1)} %bitcast.446, bf16[2048,12,64]{0,2,1:T(8,128)(2,1)} %bitcast.431), kind=kOutput, calls=%fused_computation.394 | convolution fusion | flops 830474240 | bytes 29241344 | tf_op jit(solution)/shard_map/sub | solution.py:64
  330.5 11.7 fusion.98
  355.2 14.5 %fusion.260 = (f32[12,256]{1,0:T(8,128)S(1)}, f32[12,256,2048]{2,1,0:T(8,128)}) fusion(pred[256,2048]{1,0:T(8,128)(4,1)S(1)} %copy-done.78, bf16[256,12,64]{0,2,1:T(8,128)(2,1)S(1)} %bitcast.448, bf16[2048,12,64]{0,2,1:T(8,128)(2,1)} %bitcast.433), kind=kOutput, calls=%fused_computation.392 | convolution fusion | flops 830474240 | bytes 29241344 | tf_op jit(solution)/shard_map/sub | solution.py:64
  369.7 11.5 fusion.101
  401.0 116.7 %reduce-scatter.15.cloned.1.call-done = f32[2048,96]{0,1:T(8,128)} async-done(((f32[2048,768]{0,1:T(8,128)}), f32[2048,96]{0,1:T(8,128)}) %reduce-scatter.15.cloned.1.call-update) | async-done | bytes 786448 | tf_op jit(solution)/shard_map/reduce_scatter | solution.py:302
  519.9 20.5 %reduce-scatter.17.cloned.1.call-done = f32[512,96]{0,1:T(8,128)} async-done(((f32[2048,96]{0,1:T(8,128)}), f32[512,96]{0,1:T(8,128)}) %reduce-scatter.17.cloned.1.call-update) | async-done | bytes 196624 | tf_op jit(solution)/shard_map/reduce_scatter | solution.py:308
  549.0 108.4 %all-gather.12.cloned.1.call-done = bf16[8,768,768]{1,0,2:T(8,128)(2,1)} async-done(((bf16[8,768,96]{1,0,2:T(8,128)(2,1)}), bf16[8,768,768]{1,0,2:T(8,128)(2,1)}) %all-gather.12.cloned.1.call-update) | async-done | bytes 9437200 | tf_op jit(solution)/shard_map/all_gather | solution.py:291
  657.3 18.4 %fusion.252 = (bf16[1,768,768]{1,0,2:T(2,128)(2,1)}, bf16[1,768,768]{1,0,2:T(2,128)(2,1)}, bf16[1,768,768]{1,0,2:T(2,128)(2,1)}) fusion(bf16[8,768,768]{1,0,2:T(8,128)(2,1)} %all-gather.12.cloned.1.call-done), kind=kLoop, calls=%fused_computation.384 | loop fusion | bytes 7077888 | tf_op jit(solution)/shard_map/slice | solution.py:230
  694.1 23.6 %all-gather.10.cloned.1.call-done = bf16[2048,768]{0,1:T(8,128)(2,1)} async-done(((bf16[2048,96]{0,1:T(8,128)(2,1)}), bf16[2048,768]{0,1:T(8,128)(2,1)}) %all-gather.10.cloned.1.call-update) | async-done | bytes 3145744 | tf_op jit(solution)/shard_map/all_gather | solution.py:278
  742.0 11.7 fusion.30
  753.8 17.5 %multiply_reduce_fusion = (f32[12,256]{1,0:T(8,128)}, f32[12,256,2048]{2,1,0:T(8,128)}) fusion(f32[12,256,2048]{2,1,0:T(8,128)} %get-tuple-element.203, f32[12,256]{1,0:T(8,128)S(1)} %copy-done.110, bf16[256,12,64]{0,2,1:T(8,128)(2,1)S(1)} %bitcast.482, bf16[2048,12,64]{0,2,1:T(8,128)(2,1)} %bitcast.445), kind=kOutput, calls=%fused_computation.5 | convolution fusion | flops 824177664 | bytes 53895168 | tf_op jit(solution)/shard_map/qhe,khe->hqk/dot_general | solution.py:81
  772.0 11.8 add_bitcast_fusion
  784.5 12.0 fusion.27
  804.2 16.7 %multiply_convert_fusion = bf16[12,256,2048]{2,1,0:T(8,128)(2,1)S(1)} fusion(f32[12,256,2048]{2,1,0:T(8,128)} %get-tuple-element.216, f32[12,256]{1,0:T(8,128)} %get-tuple-element.215, f32[12,256,2048]{2,1,0:T(8,128)} %get-tuple-element.203, f32[12,256]{1,0:T(8,128)} %copy-done.109), kind=kLoop, calls=%fused_computation.4 | loop fusion | flops 25165824 | bytes 62939136 | tf_op jit(solution)/shard_map/convert_element_type | solution.py:88
  828.2 17.7 %multiply_reduce_fusion.1 = (f32[12,256]{1,0:T(8,128)S(1)}, f32[12,256,2048]{2,1,0:T(8,128)}) fusion(f32[12,256,2048]{2,1,0:T(8,128)} %get-tuple-element.209, f32[12,256]{1,0:T(8,128)S(1)} %copy-done.108, bf16[256,12,64]{0,2,1:T(8,128)(2,1)S(1)} %bitcast.476, bf16[2048,12,64]{0,2,1:T(8,128)(2,1)} %bitcast.443), kind=kOutput, calls=%fused_computation.7 | convolution fusion | flops 824177664 | bytes 53895168 | tf_op jit(solution)/shard_map/qhe,khe->hqk/dot_general | solution.py:81
  846.0 16.5 %multiply_convert_fusion.1 = bf16[12,256,2048]{2,1,0:T(8,128)(2,1)S(1)} fusion(f32[12,256,2048]{2,1,0:T(8,128)} %get-tuple-element.218, f32[12,256]{1,0:T(8,128)S(1)} %get-tuple-element.217, f32[12,256,2048]{2,1,0:T(8,128)} %get-tuple-element.209, f32[12,256]{1,0:T(8,128)S(1)} %copy-done.108), kind=kLoop, calls=%fused_computation.6 | loop fusion | flops 25165824 | bytes 62939136 | tf_op jit(solution)/shard_map/convert_element_type | solution.py:88
  960.8 13.0 add.236
  1026.6 275.9 %reduce-scatter.11.cloned.1.call-done = f32[8,768,96]{1,2,0:T(8,128)} async-done(((f32[8,768,768]{1,2,0:T(8,128)}), f32[8,768,96]{1,2,0:T(8,128)}) %reduce-scatter.11.cloned.1.call-update) | async-done | bytes 2359312 | tf_op jit(solution)/shard_map/reduce_scatter | solution.py:300
  1343.5 19.3 %psum.8 = f32[3,192]{1,0:T(4,128)S(1)} all-reduce(f32[3,192]{1,0:T(4,128)S(1)} %copy.441), channel_id=1, replica_groups=mesh['dp'=8,'fsdp'=4] {'dp'}, use_global_device_ids=true, to_apply=%region_36.38 | all-reduce | flops 576 | bytes 4608 | tf_op jit(solution)/shard_map/psum | solution.py:304
  (467 shorter events, 402.5 us)
Async XLA Ops:
  8.1 25.3 %all-gather.6.cloned.1.call-start = ((), (), s32[]{:S(2)}) async-start(), calls=%async_computation.6 | async-start | bytes 1966080 | tf_op jit(solution)/shard_map/all_gather | solution.py:270
  10.5 121.5 %copy-start.44 = (bf16[2,1,256,768]{3,2,1,0:T(8,128)(2,1)S(1)}, bf16[2,1,256,768]{3,2,1,0:T(8,128)(2,1)}, u32[]{:S(2)}) copy-start(bf16[2,1,256,768]{3,2,1,0:T(8,128)(2,1)} %param.19) | copy-start | bytes 2359300
  10.5 372.9 %all-gather.8.cloned.1.call-start = ((), (), s32[]{:S(2)}) async-start(), calls=%async_computation.7 | async-start | bytes 7077888 | tf_op jit(solution)/shard_map/all_gather | solution.py:277
  35.4 30.8 %collective-permute-start = (bf16[8,768,96]{1,2,0:T(8,128)(2,1)S(1)}, bf16[8,768,96]{1,2,0:T(8,128)(2,1)S(1)}, u32[]{:S(2)}, u32[]{:S(2)}) collective-permute-start(bf16[8,768,96]{1,2,0:T(8,128)(2,1)S(1)} %copy.357), channel_id=1, source_target_pairs={{0,4},{4,8},{8,12},{12,16},{16,20},{20,24},{24,28},{28,0},{1,5},{5... | collective-permute-start | bytes 3538952 | tf_op jit(solution)/shard_map/ppermute | solution.py:29
  66.3 58.8 %collective-permute-start.1 = (bf16[8,768,96]{1,2,0:T(8,128)(2,1)S(1)}, bf16[8,768,96]{1,2,0:T(8,128)(2,1)}, u32[]{:S(2)}, u32[]{:S(2)}) collective-permute-start(bf16[8,768,96]{1,2,0:T(8,128)(2,1)S(1)} %collective-permute-done), channel_id=1, source_target_pairs={{0,4},{4,8},{8,12},{12,16},{16,20},{20,24},{24,28},{28,0},{1,5},{5... | collective-permute-start | bytes 3538952 | tf_op jit(solution)/shard_map/ppermute | solution.py:29
  74.5 443.1 %reduce-scatter.15.cloned.1.call-start = ((), (), s32[]{:S(2)}) async-start(), calls=%async_computation.12 | async-start | bytes 7077888 | tf_op jit(solution)/shard_map/reduce_scatter | solution.py:302
  74.6 55.8 %collective-permute-start.4 = (bf16[8,768,96]{1,2,0:T(8,128)(2,1)S(1)}, bf16[8,768,96]{1,2,0:T(8,128)(2,1)}, u32[]{:S(2)}, u32[]{:S(2)}) collective-permute-start(bf16[8,768,96]{1,2,0:T(8,128)(2,1)S(1)} %copy.357), channel_id=1, source_target_pairs={{0,28},{4,0},{8,4},{12,8},{16,12},{20,16},{24,20},{28,24},{1,29},{... | collective-permute-start | bytes 3538952 | tf_op jit(solution)/shard_map/ppermute | solution.py:31
  125.0 68.9 %collective-permute-start.2 = (bf16[8,768,96]{1,2,0:T(8,128)(2,1)}, bf16[8,768,96]{1,2,0:T(8,128)(2,1)}, u32[]{:S(2)}, u32[]{:S(2)}) collective-permute-start(bf16[8,768,96]{1,2,0:T(8,128)(2,1)} %collective-permute-done.1), channel_id=1, source_target_pairs={{0,4},{4,8},{8,12},{12,16},{16,20},{20,24},{24,28},{28,0},{1,5},{5... | collective-permute-start | bytes 3538952 | tf_op jit(solution)/shard_map/ppermute | solution.py:29
  130.4 69.7 %collective-permute-start.5 = (bf16[8,768,96]{1,2,0:T(8,128)(2,1)}, bf16[8,768,96]{1,2,0:T(8,128)(2,1)}, u32[]{:S(2)}, u32[]{:S(2)}) collective-permute-start(bf16[8,768,96]{1,2,0:T(8,128)(2,1)} %collective-permute-done.4), channel_id=1, source_target_pairs={{0,28},{4,0},{8,4},{12,8},{16,12},{20,16},{24,20},{28,24},{1,29},{... | collective-permute-start | bytes 3538952 | tf_op jit(solution)/shard_map/ppermute | solution.py:31
  193.9 67.7 %collective-permute-start.3 = (bf16[8,768,96]{1,2,0:T(8,128)(2,1)}, bf16[8,768,96]{1,2,0:T(8,128)(2,1)}, u32[]{:S(2)}, u32[]{:S(2)}) collective-permute-start(bf16[8,768,96]{1,2,0:T(8,128)(2,1)} %collective-permute-done.2), channel_id=1, source_target_pairs={{0,4},{4,8},{8,12},{12,16},{16,20},{20,24},{24,28},{28,0},{1,5},{5... | collective-permute-start | bytes 3538952 | tf_op jit(solution)/shard_map/ppermute | solution.py:29
  197.8 130.7 %copy-start.100 = (f32[768]{0:T(1024)}, f32[768]{0:T(1024)S(1)}, u32[]{:S(2)}) copy-start(f32[768]{0:T(1024)S(1)} %get-tuple-element.151) | copy-start | bytes 9220
  200.1 68.6 %collective-permute-start.6 = (bf16[8,768,96]{1,2,0:T(8,128)(2,1)}, bf16[8,768,96]{1,2,0:T(8,128)(2,1)S(1)}, u32[]{:S(2)}, u32[]{:S(2)}) collective-permute-start(bf16[8,768,96]{1,2,0:T(8,128)(2,1)} %collective-permute-done.5), channel_id=1, source_target_pairs={{0,28},{4,0},{8,4},{12,8},{16,12},{20,16},{24,20},{28,24},{1,29},{... | collective-permute-start | bytes 3538952 | tf_op jit(solution)/shard_map/ppermute | solution.py:31
  344.2 395.8 %copy-start.6 = (f32[256,768]{1,0:T(8,128)}, f32[256,768]{1,0:T(8,128)S(1)}, u32[]{:S(2)}) copy-start(f32[256,768]{1,0:T(8,128)S(1)} %get-tuple-element.211) | copy-start | bytes 2359300
  383.3 388.7 %copy-start.8 = (f32[256,768]{1,0:T(8,128)}, f32[256,768]{1,0:T(8,128)S(1)}, u32[]{:S(2)}) copy-start(f32[256,768]{1,0:T(8,128)S(1)} %get-tuple-element.213) | copy-start | bytes 2359300
  400.5 139.9 %copy-start.98 = (f32[512,96]{0,1:T(8,128)S(1)}, f32[512,96]{0,1:T(8,128)}, u32[]{:S(2)}) copy-start(f32[512,96]{0,1:T(8,128)} %param.30) | copy-start | bytes 589828
  400.5 139.9 %copy-start.99 = (f32[512,96]{0,1:T(8,128)S(1)}, f32[512,96]{0,1:T(8,128)}, u32[]{:S(2)}) copy-start(f32[512,96]{0,1:T(8,128)} %param.32) | copy-start | bytes 589828
  400.5 139.8 %reduce-scatter.17.cloned.1.call-start = ((), (), s32[]{:S(2)}) async-start(), calls=%async_computation.13 | async-start | bytes 983040 | tf_op jit(solution)/shard_map/reduce_scatter | solution.py:308
  517.7 139.7 %all-gather.12.cloned.1.call-start = ((), (), s32[]{:S(2)}) async-start(), calls=%async_computation.9 | async-start | bytes 10616832 | tf_op jit(solution)/shard_map/all_gather | solution.py:291
  519.9 197.9 %all-gather.10.cloned.1.call-start = ((), (), s32[]{:S(2)}) async-start(), calls=%async_computation.8 | async-start | bytes 3538944 | tf_op jit(solution)/shard_map/all_gather | solution.py:278
  548.9 448.2 %reduce-scatter.13.cloned.1.call-start = ((), (), s32[]{:S(2)}) async-start(), calls=%async_computation.11 | async-start | bytes 14155776 | tf_op jit(solution)/shard_map/reduce_scatter | solution.py:301
  783.8 518.6 %reduce-scatter.11.cloned.1.call-start = ((), (), s32[]{:S(2)}) async-start(), calls=%async_computation.10 | async-start | bytes 21233664 | tf_op jit(solution)/shard_map/reduce_scatter | solution.py:300
  973.9 368.7 %reduce-scatter.21.cloned.1.call-start = ((), (), s32[]{:S(2)}) async-start(), calls=%async_computation.15 | async-start | bytes 491520
  997.0 366.4 %all-reduce.3.cloned.1.call-start = ((), (), s32[]{:S(2)}) async-start(), calls=%async_computation.16 | async-start | bytes 3145728
  1000.9 366.3 %reduce-scatter.19.cloned.1.call-start = ((), (), s32[]{:S(2)}) async-start(), calls=%async_computation.14 | async-start | bytes 2949120
  (130 other events, 1519.8 us)
Sparse Core Ops, SparseCore 0:
  11.0 22.3 all-gather.5
  517.8 22.5 reduce-scatter.16
  1001.0 42.0 all-reduce.2
Sparse Core Ops, SparseCore 1:
  74.6 203.6 all-gather.7
  400.6 117.0 reduce-scatter.14
  520.9 136.4 all-gather.11
  659.6 58.1 all-gather.9
  783.9 205.9 reduce-scatter.12
  993.8 308.6 reduce-scatter.10
  1305.4 19.8 reduce-scatter.20
  1327.7 32.7 reduce-scatter.18
